TPU v7x, 256 devices: a whole 4x4x8 slice. The times are simulated.
256 devices in a mesh: space: 256 (over x, z, y, core).
Axes of the slice: x: 4, y: 4, z: 8, core: 2. Of those that a mesh axis runs over, the one named last changes fastest.
Arguments:
- coords: float32 [4096, 3, 128], P('space'), may hold values from -3 to 3
- force: float32 [4096, 3, 128], P('space'), may hold values from -12 to 12
- restraint: float32 [4096, 128], P('space'), may hold values from 0.25 to 4
- neighbors: int32 [4096, 32], P('space'), may hold values from 0 to 4095, as said below
- mask: int32 [4096, 32], P('space'), may hold values from 0 to 1, as said below
Outputs:
- solution_field: float32 [4096, 3, 128], P('space')
- residual: float32 [4096, 3, 128], P('space')
Inputs may be any that keep to these rules, and one draw needn't show every extreme that they name: `neighbors`: for every block b, the live entries name distinct blocks c with |c - b| <= 15; b itself is always live; if b lists c live then c lists b live; entries with mask 0 name b itself. `mask`: marks the live entries of neighbors.
All inputs are finite; a program needn't handle non-finite values.
Results may differ from a plain program's by a relative error of at most 0.0003.
Values sent between devices are 32-bit elements; how exact they have to be, the bound alone decides.
A program may use at most 64 MiB of HBM per device.

v0:
```python
import functools

import jax
import jax.numpy as jnp
from jax import lax
from jax.experimental import pallas as pl
from jax.experimental.pallas import tpu as pltpu
from jax.sharding import PartitionSpec as P

AXIS = "space"
MESH = pl.DeviceIdType.MESH
BLK = 16
BA = 128
NB = 32
PAIRS = BLK // 2
LAG = 2
LAG1 = LAG + 1
STAGES = 12
F32, BF16, F8 = jnp.float32, jnp.bfloat16, jnp.float8_e4m3fn
SHRINK = 2.0**-8
FAR = 1.5 * 2.0**63
SCALE = SHRINK * SHRINK / BA


def split2(value):
    high = value.astype(BF16).astype(F32)
    return high, value - high


def split3(value):
    high, rest = split2(value)
    middle, low = split2(rest)
    return high, middle, low


def body(
    x_acc, y_acc, z_acc, c_hbm, f_hbm, r_hbm, nb_hbm, mk_hbm, y_hbm, z_hbm, step0_ref, step1_ref, beta_ref,
    c_ref, f_ref, r_ref, nb_ref, mk_ref, in_sem, out_sem, zown,
    halo_c, halo_f, yown, yhalo, stage, enc, far_t, at, bm, feat, wh, wl, yacc, rows_v, rows_s, dmat,
    part, others, ready, c_send, c_recv, f_send, f_recv, y_send, y_recv, sum_send, sum_recv,
):
    me = lax.axis_index(AXIS)
    core, yy, zz, xx = me % 2, (me // 2) % 4, (me // 8) % 8, me // 64
    rank_a, rank_b = zz * 2 + core, xx * 4 + yy

    def member_a(rank):
        return xx * 64 + (rank // 2) * 8 + yy * 2 + rank % 2

    def member_b(rank):
        return (rank // 4) * 64 + zz * 8 + (rank % 4) * 2 + core

    before, after = (me + 255) % 256, (me + 1) % 256
    first, last = me == 0, me == 255

    pairs_in = ((c_hbm, c_ref), (f_hbm, f_ref), (r_hbm, r_ref), (nb_hbm, nb_ref), (mk_hbm, mk_ref))
    loads = [pltpu.make_async_copy(source, target, in_sem.at[k]) for k, (source, target) in enumerate(pairs_in)]
    for load in loads:
        load.start()

    barrier = pltpu.get_barrier_semaphore()
    for target in (before, after):
        pl.semaphore_signal(barrier, inc=1, device_id=(target,), device_id_type=MESH)
    for t in range(1, 16):
        pl.semaphore_signal(barrier, inc=1, device_id=(member_a((rank_a + t) % 16),), device_id_type=MESH)
        pl.semaphore_signal(barrier, inc=1, device_id=(member_b((rank_b + t) % 16),), device_id_type=MESH)

    for load in loads:
        load.wait()

    place = nb_ref[...] - me * BLK + BLK
    enc[...] = jnp.full((128, 128), -1.0, F32)
    enc[32 : 32 + BLK, 0:NB] = jnp.where(mk_ref[...] == 1, place, -1).astype(F32)
    slots = enc[...].T
    window = lax.broadcasted_iota(jnp.int32, (48, 128), 0).astype(F32)
    lane = lax.broadcasted_iota(jnp.int32, (48, 128), 1)
    hit = window == slots[0:1, :]
    for s in range(1, NB):
        hit = jnp.logical_or(hit, window == slots[s : s + 1, :])
    far_t[...] = jnp.where(jnp.logical_or(hit, jnp.logical_or(lane < 32, lane >= 32 + BLK)), 0.0, FAR)

    one = jnp.ones((BLK, BA), F32)

    turn = [0]

    def spread_rows(rows, stride):
        turn[0] = (turn[0] + 1) % STAGES
        target = stage.at[turn[0]]
        for k, row in enumerate(rows):
            target[pl.ds(k, BLK, stride=stride), :] = row
        return target

    def far_side(group, c):
        h, m, l = zip(*(split3(c[a]) for a in range(3)))
        norm = split3(c[0] * c[0] + c[1] * c[1] + c[2] * c[2])
        zero = jnp.zeros((BLK, BA), F32)
        rows = [*h, *h, *h, *m, *m, *l, *norm, one, one, one] + [zero] * 8
        source = spread_rows(rows, 32)

        def fill(e):
            block = group * BLK + e
            tall = jnp.concatenate([source[e * 32 : e * 32 + 32, :], jnp.zeros((96, BA), F32)], axis=0)
            at[block * BA : (block + 1) * BA, :] = (tall.T + far_t[block : block + 1, :]).astype(BF16)

        return fill

    def near_side(c):
        h, m, l = zip(*(split3(c[a]) for a in range(3)))
        norm = split3(1.0 + (c[0] * c[0] + c[1] * c[1] + c[2] * c[2]))
        zero = jnp.zeros((BLK, BA), F32)
        h, m, l = ([-2.0 * SHRINK * v for v in vs] for vs in (h, m, l))
        norm = [SHRINK * v for v in norm]
        shrink = jnp.full((BLK, BA), SHRINK, F32)
        rows = [*h, *m, *l, *h, *m, *h, shrink, shrink, shrink, *norm] + [zero] * 8
        source = spread_rows(rows, 32)
        row = lax.broadcasted_iota(jnp.int32, (96, BA), 0)
        for b in range(BLK):
            lanes = slice((b % 2) * BA, (b % 2 + 1) * BA)
            full = jnp.concatenate([source[b * 32 : b * 32 + 32, :], jnp.where(row == b, 1.0, 0.0)], axis=0)
            bm[b // 2, :, lanes] = full.astype(BF16)

    def store_features(group, values, high_row, low_row):
        highs, lows = zip(*(split2(v) for v in values))
        sources = [(spread_rows(split, 16), row) for split, row in ((highs, high_row), (lows, low_row))]

        def fill(e):
            lanes = slice((group * BLK + e) * BA, (group * BLK + e + 1) * BA)
            for source, row in sources:
                feat[row : row + 16, lanes] = source[e * 16 : e * 16 + 16, :].astype(BF16)

        return fill

    def field_features(group, c, v):
        p = c[0] * v[0] + c[1] * v[1] + c[2] * v[2]
        values = [c[a] * p for a in range(3)] + [p] + [v[b] for b in range(3)]
        values += [c[a] * v[b] for a in range(3) for b in range(3)]
        return store_features(group, values, 16, 0)

    def place_features(group, c):
        zero = jnp.zeros((BLK, BA), F32)
        values = [one, c[0], c[1], c[2], c[0] * c[0], c[1] * c[1], c[2] * c[2]]
        values += [c[0] * c[1], c[0] * c[2], c[1] * c[2]] + [zero] * 6
        return store_features(group, values, 32, 48)

    def fill_all(*fills):
        for e in range(BLK):
            for fill in fills:
                fill(e)

    def tiles_of(p, inside):
        if inside:
            return [((BLK + 2 * k, BLK + 2 * k + 1), k) for k in range(8)]
        low = [(e, e + 1) for e in range(2 * p + 2, BLK, 2)]
        up = [(e, e + 1) for e in range(2 * BLK, 2 * BLK + 2 * p, 2)]
        return [(blocks, 8 + k) for k, blocks in enumerate(low + up + [(2 * p + 1, 2 * BLK + 2 * p)])]

    def lanes_of(rows, blocks):
        i, j = blocks
        if j == i + 1:
            return feat[rows, i * BA : (j + 1) * BA]
        return jnp.concatenate([feat[rows, e * BA : (e + 1) * BA] for e in blocks], axis=1)

    zeros = jnp.zeros((BA, BA), BF16)
    register = [0, 0]

    def push(q, tile):
        register[q] = 1 - register[q]
        pltpu.matmul_push_rhs(tile, staging_register=register[q], mxu_index=q)
        return register[q]

    steps = [(pair, t) for pair in range(PAIRS // 2) for t in range(8)]

    def build(inside, ahead=None, collected=None):
        lists = [tiles_of(p, inside) for p in range(PAIRS)]

        def start(q, i):
            pair, t = steps[i]
            p = 2 * pair + q
            wide = jnp.concatenate([bm[p], jnp.zeros((BA, 2 * BA), BF16)], axis=0)
            staged = push(q, wide)
            for k, e in enumerate(lists[p][t][0]):
                lhs = jnp.concatenate([at[e * BA : (e + 1) * BA, :], zeros], axis=1)
                pltpu.matmul_acc_lhs(x_acc[q][i % LAG1][k], lhs, load_staged_rhs=staged if k == 0 else None)

        def finish(q, i):
            pair, t = steps[i]
            p = 2 * pair + q
            blocks, slot = lists[p][t]
            for k in range(2):
                x = pltpu.matmul_pop(x_acc[q][i % LAG1][k])
                w = 1.0 / (x * x)
                high = w.astype(BF16)
                low = (w - high.astype(F32)).astype(F8)
                rows = slice(slot * 2 * BA + k * BA, slot * 2 * BA + (k + 1) * BA)
                wh[p, rows, :] = high
                wl[p, rows, :] = low
            acc_h, acc_l = y_acc[q][pair % 2]
            tile = slice(slot * 2 * BA, (slot + 1) * 2 * BA)
            staged = push(q, wh[p, tile, :])
            pltpu.matmul_acc_lhs(acc_h, lanes_of(slice(0, 64), blocks), load_staged_rhs=staged)
            staged = push(q, wl[p, tile, :])
            pltpu.matmul_acc_lhs(acc_l, lanes_of(slice(16, 48), blocks), load_staged_rhs=staged)

        def collect(pair):
            for q in range(2):
                p = 2 * pair + q
                acc_h, acc_l = y_acc[q][pair % 2]
                total_h, total_l = pltpu.matmul_pop(acc_h), pltpu.matmul_pop(acc_l)
                if inside:
                    yacc[p, 0:64, :] = total_h
                    yacc[p, 64:96, :] = total_l
                    continue
                total_h += yacc[p, 0:64, :]
                total_l += yacc[p, 64:96, :]
                value = total_h[0:16] + total_h[16:32] + total_l[0:16]
                still = total_h[32:48] + total_h[48:64] + total_l[16:32]
                for k in range(2):
                    rows = slice((2 * p + k) * 16, (2 * p + k + 1) * 16)
                    rows_v[rows, :] = value[:, k * BA : (k + 1) * BA]
                    rows_s[rows, :] = still[:, k * BA : (k + 1) * BA]

        for i in range(len(steps) + LAG):
            if ahead is not None:
                ahead(i)
            for q in range(2):
                if i < len(steps):
                    start(q, i)
            for q in range(2):
                if i >= LAG:
                    finish(q, i - LAG)
            if i >= LAG + 9 and (i - LAG - 9) % 8 == 0:
                collect((i - LAG - 9) // 8)
                if collected is not None:
                    collected((i - LAG - 9) // 8)
        collect(PAIRS // 2 - 1)
        if collected is not None:
            collected(PAIRS // 2 - 1)

    def product(phase):
        lists = [tiles_of(p, phase == 0) for p in range(PAIRS)]
        if phase > 0:
            early = [[tile for tile in tiles if all(e % BLK < 8 for e in tile[0])] for tiles in lists]
            lists = early if phase == 1 else [
                [tile for tile in tiles if tile not in first] for tiles, first in zip(lists, early)
            ]

        def collect(pair):
            for q in range(2):
                p = 2 * pair + q
                acc_h, acc_l = z_acc[q][pair % 2]
                total_h, total_l = pltpu.matmul_pop(acc_h), pltpu.matmul_pop(acc_l)
                value = total_h[0:16] + total_h[16:32] + total_l
                if phase > 0:
                    value += yacc[p, 0:16, :]
                if phase < 2:
                    yacc[p, 0:16, :] = value
                    continue
                for k in range(2):
                    rows_v[(2 * p + k) * 16 : (2 * p + k + 1) * 16, :] = value[:, k * BA : (k + 1) * BA]

        count = len(lists[0])
        assert all(len(tiles) == count for tiles in lists)
        for i in range(PAIRS // 2 * count):
            pair, t = i // count, i % count
            for q in range(2):
                p = 2 * pair + q
                blocks, slot = lists[p][t]
                acc_h, acc_l = z_acc[q][pair % 2]
                rows = slice(slot * 2 * BA, (slot + 1) * 2 * BA)
                staged = push(q, wh[p, rows, :])
                pltpu.matmul_acc_lhs(acc_h, lanes_of(slice(0, 32), blocks), load_staged_rhs=staged)
                staged = push(q, wl[p, rows, :])
                pltpu.matmul_acc_lhs(acc_l, lanes_of(slice(16, 32), blocks), load_staged_rhs=staged)
            if i > count and i % count == 1:
                collect(i // count - 1)
        collect(PAIRS // 2 - 1)

    def combine(half, c, v):
        t = [rows_v[pl.ds(k + half * 128, 8, stride=16), :] for k in range(16)]
        cv = c[0] * t[4] + c[1] * t[5] + c[2] * t[6]
        out = []
        for a in range(3):
            gone = t[a] - c[a] * t[3] + c[a] * cv
            gone = gone - (c[0] * t[7 + 3 * a] + c[1] * t[8 + 3 * a] + c[2] * t[9 + 3 * a])
            kept = sum(dmat[half, PACK[a][b]] * v[b] for b in range(3))
            out.append(kept - gone * SCALE)
        return out

    c = [c_ref[a] for a in range(3)]
    f = [f_ref[a] for a in range(3)]
    near_side(c)
    fill_all(far_side(1, c), field_features(1, c, f), place_features(1, c))

    pl.semaphore_wait(barrier, 32)

    def exchange(source, target, send, recv):
        up, down = (
            pltpu.make_async_remote_copy(
                src_ref=source, dst_ref=target.at[k], send_sem=send.at[k], recv_sem=recv.at[k],
                device_id=(neighbour,), device_id_type=MESH,
            )
            for k, neighbour in ((0, after), (1, before))
        )

        @pl.when(jnp.logical_not(last))
        def _():
            up.start()

        @pl.when(jnp.logical_not(first))
        def _():
            down.start()

        @pl.when(first)
        def _():
            target[0] = jnp.zeros(target.shape[1:], F32)

        @pl.when(last)
        def _():
            target[1] = jnp.zeros(target.shape[1:], F32)

        def finish():
            @pl.when(jnp.logical_not(last))
            def _():
                up.wait_send()
                down.wait_recv()

            @pl.when(jnp.logical_not(first))
            def _():
                down.wait_send()
                up.wait_recv()

        return finish

    finish_c = exchange(c_ref, halo_c, c_send, c_recv)
    finish_f = exchange(f_ref, halo_f, f_send, f_recv)
    for t in range(1, 16):
        pl.semaphore_signal(ready, inc=1, device_id=(member_b((rank_b + t) % 16),), device_id_type=MESH)

    build(True)

    finish_c()
    finish_f()
    hc = [[halo_c[side, a] for a in range(3)] for side in range(2)]
    far_fill, field_fill = {}, {}

    def open_far(side):
        far_fill[side] = far_side(2 * side, hc[side])

    def open_fields(side):
        hf = [halo_f[side, a] for a in range(3)]
        fills = (field_features(2 * side, hc[side], hf), place_features(2 * side, hc[side]))
        field_fill[side] = lambda e: [fill(e) for fill in fills]

    def fill_blocks(fills, side, *blocks):
        for e in blocks:
            fills[side](e)

    def ahead(i):
        if i == 0:
            open_far(0)
            fill_blocks(far_fill, 0, 2, 3, 4, 5)
        if i == 1:
            fill_blocks(far_fill, 0, 6, 7)
            open_fields(0)
            fill_blocks(field_fill, 0, 2, 3, 4, 5)
        if i == 2:
            fill_blocks(far_fill, 0, 8, 9)
            fill_blocks(field_fill, 0, 6, 7)
            open_far(1)
        if i == 3:
            fill_blocks(far_fill, 0, 10, 11)
            fill_blocks(field_fill, 0, 8, 9)
            fill_blocks(far_fill, 1, 0, 1, 2)
        if i == 4:
            fill_blocks(far_fill, 0, 12, 13)
            fill_blocks(field_fill, 0, 10, 11)
            fill_blocks(far_fill, 1, 3, 4, 5, 6)
            open_fields(1)
        if i == 5:
            fill_blocks(far_fill, 0, 14, 15, 1)
            fill_blocks(field_fill, 0, 12, 13)
            fill_blocks(far_fill, 1, 7, 8, 9, 10)
            fill_blocks(field_fill, 1, 0, 1, 2, 3)
        if i == 6:
            fill_blocks(far_fill, 1, 11, 12, 13, 14)
            fill_blocks(field_fill, 0, 14, 15, 1)
            fill_blocks(field_fill, 1, 4, 5, 6, 7, 8)
        if i == 7:
            fill_blocks(field_fill, 1, 9, 10, 11, 12, 13, 14)

    finishes, copies_out = [], []

    def first_product(pair):
        if pair % 2 == 0:
            return
        half = pair // 2
        rows = slice(8 * half, 8 * half + 8)
        ch = [c_ref[a, rows] for a in range(3)]
        fh = [f_ref[a, rows] for a in range(3)]
        s = [rows_s[pl.ds(k + half * 128, 8, stride=16), :] for k in range(10)]
        for a, b, k in ((0, 0, 4), (1, 1, 5), (2, 2, 6), (0, 1, 7), (0, 2, 8), (1, 2, 9)):
            entry = (s[k] - ch[a] * s[1 + b] - ch[b] * s[1 + a] + ch[a] * ch[b] * s[0]) * SCALE
            dmat[half, PACK[a][b]] = entry + r_ref[rows] if a == b else entry
        value = combine(half, ch, fh)
        for a in range(3):
            yown[half, a] = value[a]
        finishes.append(exchange(yown.at[half], yhalo.at[half], y_send.at[half], y_recv.at[half]))
        copies_out.append(pltpu.make_async_copy(yown.at[half], y_hbm.at[:, rows], out_sem.at[half]))
        copies_out[-1].start()

    build(False, ahead, first_product)

    y = [jnp.concatenate([yown[0, a], yown[1, a]], axis=0) for a in range(3)]
    fill_all(field_features(1, c, y))
    product(0)
    for half in range(2):
        finishes[half]()
        for side in range(2):
            blank = jnp.zeros((8, BA), F32)
            parts = [[yhalo[half, side, a], blank] for a in range(3)]
            hy = [jnp.concatenate(part if half == 0 else part[::-1], axis=0) for part in parts]
            fill = field_features(2 * side, hc[side], hy)
            for e in range(8 * half, 8 * half + 8):
                fill(e)
        product(1 + half)
    halves = [
        combine(half, [c[a][8 * half : 8 * half + 8] for a in range(3)], [yown[half, a] for a in range(3)])
        for half in range(2)
    ]
    z = [jnp.concatenate([halves[0][a], halves[1][a]], axis=0) for a in range(3)]
    for a in range(3):
        zown[a] = z[a]
    z_out = pltpu.make_async_copy(zown, z_hbm, out_sem.at[2])
    z_out.start()

    def inner(u, v):
        return jnp.sum(u[0] * v[0] + u[1] * v[1] + u[2] * v[2], axis=0, keepdims=True)

    sums = [inner(f, f), inner(f, y), inner(y, y), inner(f, z), inner(y, z)]
    tile = jnp.concatenate(sums + [jnp.zeros((3, BA), F32)], axis=0)
    for shift in (64, 32, 16):
        tile = tile + pltpu.roll(tile, shift, 1)
    row8 = lax.broadcasted_iota(jnp.int32, (8, BA), 0)
    lane8 = lax.broadcasted_iota(jnp.int32, (8, BA), 1)
    packed = jnp.sum(jnp.where(lane8 // 16 == row8, tile, 0.0), axis=0, keepdims=True)

    part[0] = packed
    pl.semaphore_wait(ready, 15)
    xs = [(xx + d) % 4 * 64 for d in range(4)]
    zs = [(zz + d) % 8 * 8 for d in range(8)]
    ys = [(yy + d) % 4 * 2 for d in range(4)]
    cores = (core, 1 - core)
    hops = sorted(
        (-min(dx, 4 - dx) - min(dz, 8 - dz) - min(dy, 4 - dy), -dc, dx, dz, dy)
        for dx in range(4) for dz in range(8) for dy in range(4) for dc in range(2)
    )
    for _, dc, dx, dz, dy in hops[:-1]:
        pltpu.make_async_remote_copy(
            src_ref=part.at[0], dst_ref=others.at[me], send_sem=sum_send.at[0], recv_sem=sum_recv.at[0],
            device_id=(xs[dx] + zs[dz] + ys[dy] + cores[-dc],), device_id_type=MESH,
        ).start()
    others[me] = packed
    pltpu.make_async_copy(others.at[pl.ds(1, 255)], others.at[pl.ds(1, 255)], sum_recv.at[0]).wait()
    pltpu.make_async_copy(others.at[pl.ds(1, 255)], others.at[pl.ds(1, 255)], sum_send.at[0]).wait()
    packed = jnp.sum(others[:, 0, :], axis=0, keepdims=True)

    spread = jnp.broadcast_to(packed, (8, BA))
    first16 = lax.broadcasted_iota(jnp.int32, (8, BA), 1) < 16
    ff, fy, yy_, fz, yz = (
        jnp.where(first16, spread if k == 0 else pltpu.roll(spread, BA - 16 * k, 1), 0.0) for k in range(5)
    )

    def whole(value):
        return jnp.sum(value, axis=1, keepdims=True)

    ff_all = whole(ff)
    step0 = ff_all / whole(fy)
    norm1 = whole((ff - step0 * fy) - step0 * (fy - step0 * yy_))
    beta = norm1 / ff_all
    ry, fq = fy - step0 * yy_, fy - step0 * fz
    rq = fq - step0 * (yy_ - step0 * yz)
    step1 = norm1 / whole(rq + beta * (ry + fq) + beta * beta * fy)
    for target, value in ((step0_ref, step0), (step1_ref, step1), (beta_ref, beta)):
        target[...] = jnp.broadcast_to(value[0:1], (1, BA))
    for copy in (*copies_out, z_out):
        copy.wait()


def kernel(*refs):
    def accumulator(q, rows):
        return pltpu.ACC(q)((rows, 2 * BA), F32)

    def both(x_acc, y_acc, low_acc):
        z_acc = [[(y_acc[q][k][1], low_acc[q][k]) for k in range(2)] for q in range(2)]
        body(x_acc, y_acc, z_acc, *refs)

    pl.run_scoped(
        both,
        [[[accumulator(q, BA) for _ in range(2)] for _ in range(LAG1)] for q in range(2)],
        [[(accumulator(q, 64), accumulator(q, 32)) for _ in range(2)] for q in range(2)],
        [[accumulator(q, 16) for _ in range(2)] for q in range(2)],
    )


PACK = ((0, 3, 4), (3, 1, 5), (4, 5, 2))


def last_step(f_ref, y_ref, z_ref, step0_ref, step1_ref, beta_ref, sol_ref, res_ref):
    step0, step1, beta = (jnp.broadcast_to(ref[...], (BLK, BA)) for ref in (step0_ref, step1_ref, beta_ref))
    for a in range(3):
        first = f_ref[a] - step0 * y_ref[a]
        along = (y_ref[a] - step0 * z_ref[a]) + beta * y_ref[a]
        direction = first + beta * f_ref[a]
        sol_ref[a] = step0 * f_ref[a] + step1 * direction
        res_ref[a] = first - step1 * along


def per_device(coords, force, restraint, neighbors, mask):
    vmem = pl.BlockSpec(memory_space=pltpu.VMEM)
    anywhere = pl.BlockSpec(memory_space=pl.ANY)
    field = jax.ShapeDtypeStruct((3, BLK, BA), F32)
    row = jax.ShapeDtypeStruct((1, BA), F32)
    dma = pltpu.SemaphoreType.DMA
    y, z, step0, step1, beta = pl.pallas_call(
        kernel,
        out_shape=(field, field, row, row, row),
        in_specs=[anywhere] * 5,
        out_specs=(anywhere, anywhere, vmem, vmem, vmem),
        scratch_shapes=[
            pltpu.VMEM((3, BLK, BA), F32),
            pltpu.VMEM((3, BLK, BA), F32),
            pltpu.VMEM((BLK, BA), F32),
            pltpu.VMEM((BLK, NB), jnp.int32),
            pltpu.VMEM((BLK, NB), jnp.int32),
            dma((5,)),
            dma((3,)),
            pltpu.VMEM((3, BLK, BA), F32),
            pltpu.VMEM((2, 3, BLK, BA), F32),
            pltpu.VMEM((2, 3, BLK, BA), F32),
            pltpu.VMEM((2, 3, 8, BA), F32),
            pltpu.VMEM((2, 2, 3, 8, BA), F32),
            pltpu.VMEM((STAGES, 32 * BLK, BA), F32),
            pltpu.VMEM((128, 128), F32),
            pltpu.VMEM((48, 128), F32),
            pltpu.VMEM((48 * BA, 128), BF16),
            pltpu.VMEM((PAIRS, 128, 2 * BA), BF16),
            pltpu.VMEM((64, 48 * BA), BF16),
            pltpu.VMEM((PAIRS, 32 * BA, 2 * BA), BF16),
            pltpu.VMEM((PAIRS, 32 * BA, 2 * BA), F8),
            pltpu.VMEM((PAIRS, 96, 2 * BA), F32),
            pltpu.VMEM((16 * BLK, BA), F32),
            pltpu.VMEM((16 * BLK, BA), F32),
            pltpu.VMEM((2, 6, 8, BA), F32),
            pltpu.VMEM((1, 1, BA), F32),
            pltpu.VMEM((256, 1, BA), F32),
            pltpu.SemaphoreType.REGULAR,
            dma((2,)), dma((2,)), dma((2,)), dma((2,)), dma((2, 2)), dma((2, 2)), dma((2,)), dma((2,)),
        ],
        compiler_params=pltpu.CompilerParams(collective_id=0, has_side_effects=True),
    )(coords.transpose(1, 0, 2), force.transpose(1, 0, 2), restraint, neighbors, mask)
    solution_field, residual = pl.pallas_call(
        last_step,
        out_shape=(field, field),
        in_specs=[vmem] * 6,
        out_specs=(vmem, vmem),
    )(force.transpose(1, 0, 2), y, z, step0, step1, beta)
    return solution_field.transpose(1, 0, 2), residual.transpose(1, 0, 2)


def solution(mesh):
    return jax.shard_map(
        per_device,
        mesh=mesh,
        in_specs=(P(AXIS, None, None), P(AXIS, None, None), P(AXIS, None), P(AXIS, None), P(AXIS, None)),
        out_specs=(P(AXIS, None, None), P(AXIS, None, None)),
        check_vma=False,
    )
```

profile of v0, /device:TPU:1, one launch (start us, length us, event | category | flops | bytes accessed | tf_op | source)
XLA Modules:
  0.0 36.5 jit_solution(4820343001768155496)
XLA Ops:
  0.6 34.5 %shard_map.68 = (f32[3,16,128]{2,1,0:T(8,128)}, f32[3,16,128]{2,1,0:T(8,128)}, f32[1,128]{1,0:T(1,128)}, f32[1,128]{1,0:T(1,128)}, f32[1,128]{1,0:T(1,128)}) custom-call(f32[3,16,128]{2,1,0:T(8,128)} %bitcast.6, f32[3,16,128]{2,1,0:T(8,128)} %bitcast.4, f32[16,128]{1,0:T(8,128)} %refs_2_.1, s32[16,32]{1,0:T(8,128)} %refs_3_.1, s32[16,32]{1,0:T(8,128)} %refs_4_.1), custom_call_target="tpu_custom_call" | custom-call | tf_op jit(solution)/shard_map/pallas_call | solution.py:523
  35.1 1.4 %shard_map.69 = (f32[3,16,128]{2,1,0:T(8,128)}, f32[3,16,128]{2,1,0:T(8,128)}) custom-call(f32[3,16,128]{2,1,0:T(8,128)} %bitcast.5, f32[3,16,128]{2,1,0:T(8,128)} %get-tuple-element.9.y_ref, f32[3,16,128]{2,1,0:T(8,128)} %get-tuple-element.10.z_ref, f32[1,128]{1,0:T(1,128)} %get-tuple-element.11.step0_ref, f32[1,128]{1,0:T(1,128)} %get-tuple-element.12.step1_ref, ...), custom_call_target="tpu_custom_call" | custom-call | tf_op jit(solution)/shard_map/pallas_call | solution.py:560
where the time goes:
time: 36.7 us; the launch traced here: 36.5 us
  Pallas kernels  35.9 us (98%)
  between operations  0.64 us (2%)
    pallas_call x1, Pallas kernels, per_device(): pl.pallas_call(kernel, out_shape=(field, field, row, row, row), in_specs=...  34.5 us
    pallas_call x1, Pallas kernels, per_device(): pl.pallas_call(last_step, out_shape=(field, field), in_specs=[vmem] * 6,...  1.41 us

commit v1 on v0

--- a/solution.py
+++ b/solution.py
@@ -189,9 +189,9 @@
                 x = pltpu.matmul_pop(x_acc[q][i % LAG1][k])
                 w = 1.0 / (x * x)
                 high = w.astype(BF16)
-                low = (w - high.astype(F32)).astype(F8)
                 rows = slice(slot * 2 * BA + k * BA, slot * 2 * BA + (k + 1) * BA)
                 wh[p, rows, :] = high
+                low = (w - wh[p, rows, :].astype(F32)).astype(F8)
                 wl[p, rows, :] = low
             acc_h, acc_l = y_acc[q][pair % 2]
             tile = slice(slot * 2 * BA, (slot + 1) * 2 * BA)
@@ -338,7 +338,6 @@
     build(True)
 
     finish_c()
-    finish_f()
     hc = [[halo_c[side, a] for a in range(3)] for side in range(2)]
     far_fill, field_fill = {}, {}
 
@@ -360,6 +359,7 @@
             fill_blocks(far_fill, 0, 2, 3, 4, 5)
         if i == 1:
             fill_blocks(far_fill, 0, 6, 7)
+            finish_f()
             open_fields(0)
             fill_blocks(field_fill, 0, 2, 3, 4, 5)
         if i == 2:

time: 36.7 us -> 36.1 us (0.984)
  Pallas kernels: 35.9 us -> 35.2 us
    pallas_call x1, Pallas kernels: 34.5 us -> 33.8 us  [per_device(): pl.pallas_call(kernel, out_shape=(field, field, row, row, row), in_specs=...]
where the time goes in v1:
time: 36.1 us; the launch traced here: 35.9 us
  Pallas kernels  35.2 us (98%)
  between operations  0.64 us (2%)
    pallas_call x1, Pallas kernels, per_device(): pl.pallas_call(kernel, out_shape=(field, field, row, row, row), in_specs=...  33.8 us
    pallas_call x1, Pallas kernels, per_device(): pl.pallas_call(last_step, out_shape=(field, field), in_specs=[vmem] * 6,...  1.41 us

profile of v1, /device:TPU:1, one launch (start us, length us, event | category | flops | bytes accessed | tf_op | source)
XLA Modules:
  0.0 35.9 jit_solution(4108243988981765630)
XLA Ops:
  0.6 33.8 %shard_map.68 = (f32[3,16,128]{2,1,0:T(8,128)}, f32[3,16,128]{2,1,0:T(8,128)}, f32[1,128]{1,0:T(1,128)}, f32[1,128]{1,0:T(1,128)}, f32[1,128]{1,0:T(1,128)}) custom-call(f32[3,16,128]{2,1,0:T(8,128)} %bitcast.6, f32[3,16,128]{2,1,0:T(8,128)} %bitcast.4, f32[16,128]{1,0:T(8,128)} %refs_2_.1, s32[16,32]{1,0:T(8,128)} %refs_3_.1, s32[16,32]{1,0:T(8,128)} %refs_4_.1), custom_call_target="tpu_custom_call" | custom-call | tf_op jit(solution)/shard_map/pallas_call | solution.py:523
  34.4 1.4 %shard_map.69 = (f32[3,16,128]{2,1,0:T(8,128)}, f32[3,16,128]{2,1,0:T(8,128)}) custom-call(f32[3,16,128]{2,1,0:T(8,128)} %bitcast.5, f32[3,16,128]{2,1,0:T(8,128)} %get-tuple-element.9.y_ref, f32[3,16,128]{2,1,0:T(8,128)} %get-tuple-element.10.z_ref, f32[1,128]{1,0:T(1,128)} %get-tuple-element.11.step0_ref, f32[1,128]{1,0:T(1,128)} %get-tuple-element.12.step1_ref, ...), custom_call_target="tpu_custom_call" | custom-call | tf_op jit(solution)/shard_map/pallas_call | solution.py:560
